TPU v7x, 32 devices: a whole 2x2x4 slice. The times are simulated.
32 devices in a mesh: member: 2 (over x), lat: 16 (over z, y, core).
Axes of the slice: x: 2, y: 2, z: 4, core: 2. Of those that a mesh axis runs over, the one named last changes fastest.
Arguments:
- field: bfloat16 [192, 1440, 256], P(('member', 'lat')), parts along dimension 0, may hold values from -3000 to 3000
- gain: float32 [256], replicated, may hold values from 0.1 to 1.9
- slot_wave: int32 [96], replicated, may hold values from 0 to 96, as said below
- legendre: bfloat16 [96, 96, 96], P('lat'), may hold values from -0.625 to 0.625
- mixing: bfloat16 [96, 2, 256, 256], P('lat'), may hold values from -0.25 to 0.25
Outputs:
- result: bfloat16 [192, 1440, 256], P(('member', 'lat')), parts along dimension 0
There are 2 independent parts, one for each index of `member`. A program takes and returns all parts, laid end to end along the dimension named above; an argument that names none is the same for every part. Nothing has to cross between parts.
Inputs may be any that keep to these rules, and one draw needn't show every extreme that they name: `slot_wave`: each wavenumber 0 to 95 stands in exactly one slot and every other slot holds 96; slots 2k and 2k+1 of one lat index hold wavenumbers adding up to (4k+2)16 - 1 where both are below 96.
All inputs are finite; a program needn't handle non-finite values.
Results may differ from a plain program's by a relative error of at most 0.0085.
Values may be sent and summed in bfloat16 or wider, within the bound.
No kernel may reach another device: no remote copies, remote signals or barrier semaphores. Data moves between devices by JAX's collectives and lax.ppermute only.
A program may use at most 64 MiB of HBM per device.

v0:
```python
import math
import jax
import jax.numpy as jnp
from jax import lax
from jax.sharding import PartitionSpec as P


def phase_tables(waves, width):
    points = jnp.arange(width, dtype=jnp.int32)
    phase = (waves[:, None] * points[None, :] % width).astype(jnp.float32) * (2.0 * math.pi / width)
    return (jnp.cos(phase), jnp.sin(phase))


def block_weight(mixing):
    real_part = mixing[:, 0]
    imag_part = mixing[:, 1]
    upper = jnp.concatenate([real_part, imag_part], axis=2)
    lower = jnp.concatenate([-imag_part, real_part], axis=2)
    return jnp.concatenate([upper, lower], axis=1)


def per_device(field, gain, slot_wave, legendre, mixing):
    lat_count = lax.axis_size("lat")
    lat_dev, width, chans = field.shape
    slot_dev, degs, nlat = legendre.shape
    count = float(lat_dev * lat_count * width)
    values = field.astype(jnp.float32)
    local_sum = jnp.sum(values, axis=(0, 1))
    local_sq = jnp.sum(values * values, axis=(0, 1))
    total, squares = lax.psum((local_sum, local_sq), "lat")
    mean = total / count
    var = squares / count - mean * mean
    normed = ((values - mean) * (gain / jnp.sqrt(var + 1e-05))).astype(jnp.bfloat16)
    cosine, sine = phase_tables(slot_wave, width)
    forward = jnp.stack([cosine, -sine]).astype(jnp.bfloat16).reshape(2, lat_count, slot_dev, width)
    weight_m = jnp.where(slot_wave == 0, 1.0, 2.0).astype(jnp.float32)[:, None]
    inverse = jnp.stack([weight_m * cosine, -weight_m * sine]).astype(jnp.bfloat16)
    inv_root = 1.0 / math.sqrt(width)
    spectrum = (
        jnp.einsum("anc,rdjn->dajrc", normed, forward, preferred_element_type=jnp.float32)
        * inv_root
    )
    spectrum = spectrum.astype(jnp.bfloat16).reshape(lat_count, lat_dev, slot_dev, 2 * chans)
    arrived = lax.all_to_all(spectrum, "lat", split_axis=0, concat_axis=1, tiled=True)[0]
    mine = lax.dynamic_slice_in_dim(slot_wave, lax.axis_index("lat") * slot_dev, slot_dev, 0)
    big = block_weight(mixing)
    lat_scale = math.sqrt(nlat / degs)
    degrees = jnp.arange(degs, dtype=jnp.int32)
    coef = jnp.einsum("jlt,tjc->jlc", legendre, arrived, preferred_element_type=jnp.float32)
    coef = jnp.where((degrees[None, :] >= mine[:, None])[:, :, None], coef, 0.0).astype(
        jnp.bfloat16
    )
    mixed = jnp.einsum("jlc,jcd->jld", coef, big, preferred_element_type=jnp.float32).astype(
        jnp.bfloat16
    )
    back = (
        jnp.einsum("jlt,jld->tjd", legendre, mixed, preferred_element_type=jnp.float32) * lat_scale
    )
    back = back.astype(jnp.bfloat16)
    back = back.reshape(lat_count, lat_dev, slot_dev, 2 * chans)
    returned = lax.all_to_all(back, "lat", split_axis=0, concat_axis=2, tiled=True)[0]
    returned = returned.reshape(lat_dev, slot_dev * lat_count, 2, chans)
    filtered = (
        jnp.einsum("akrc,rkn->anc", returned, inverse, preferred_element_type=jnp.float32)
        * inv_root
    )
    return (normed.astype(jnp.float32) + filtered).astype(jnp.bfloat16)


def solution(mesh):
    return jax.shard_map(
        per_device,
        mesh=mesh,
        in_specs=(
            P(("member", "lat"), None, None),
            P(),
            P(),
            P("lat", None, None),
            P("lat", None, None, None),
        ),
        out_specs=P(("member", "lat"), None, None),
        check_vma=False,
    )
```

profile of v0, /device:TPU:9, one launch (start us, length us, event | category | flops | bytes accessed | tf_op | source)
XLA Modules:
  0.0 103.9 jit_solution(11740767256744801090)
XLA Ops:
  0.0 3.5 %convert_reduce_fusion = (f32[256]{0:T(256)S(1)}, f32[256]{0:T(256)S(1)}) fusion(bf16[6,1440,256]{2,1,0:T(8,128)(2,1)} %param.5), kind=kLoop, calls=%fused_computation.2 | loop fusion | flops 8846848 | bytes 4425728 | tf_op jit(solution)/shard_map/reduce_sum | solution.py:28
  3.5 0.1 mul.154
  3.6 0.1 copy.23
  3.7 2.8 %cosine_convert_fusion = (bf16[1,16,6,1440]{3,1,2,0:T(8,128)(2,1)S(1)}, bf16[1,16,6,1440]{3,1,2,0:T(8,128)(2,1)S(1)}) fusion(s32[16,6]{0,1:T(8,128)S(1)} %copy.23), kind=kLoop, calls=%fused_computation.44 | loop fusion | flops 1658880 | bytes 553344 | tf_op jit(solution)/shard_map/convert
  6.5 22.3 %all-reduce = (f32[256]{0:T(256)S(1)}, f32[256]{0:T(256)S(1)}) all-reduce(f32[256]{0:T(256)S(1)} %get-tuple-element.6, f32[256]{0:T(256)S(1)} %get-tuple-element.5), channel_id=1, replica_groups=mesh['member'=2,'lat'=16] {'lat'}, use_global_device_ids=true, to_apply=%region_3.0 | all-reduce | flops 512 | bytes 4096 | tf_op jit(solution)/shard_map/psum | solution.py:30
  28.9 3.6 %fusion.26 = bf16[16,6,6,2,256]{4,0,1,2,3:T(8,128)(2,1)S(1)} fusion(f32[256]{0:T(256)S(1)} %get-tuple-element.14, f32[256]{0:T(256)S(1)} %get-tuple-element.13, bf16[6,1440,256]{2,1,0:T(8,128)(2,1)} %param.5, bf16[1,16,6,1440]{3,1,2,0:T(8,128)(2,1)S(1)} %get-tuple-element.12, bf16[1,16,6,1440]{3,1,2,0:T(8,128)(2,1)S(1)} %get-tuple-element.11), kind=kOutput, calls=%fused_computation.26 | convolution fusion | flops 859889664 | bytes 5568512 | tf_op jit(solution)/shard_map/anc,rdjn->dajrc/dot_general | solution.py:40
  32.5 0.0 copy-start.1
  32.5 0.6 copy.37
  33.1 1.3 %reshape.223 = bf16[16,6,6,512]{3,2,1,0:T(8,128)(2,1)} reshape(bf16[16,6,6,2,256]{4,3,2,1,0:T(2,128)(2,1)S(1)} %copy.37) | data formatting | bytes 1179648 | tf_op jit(solution)/shard_map/reshape | solution.py:43
  34.4 15.3 %all-to-all-start = ((bf16[16,6,6,512]{3,2,1,0:T(8,128)(2,1)}), bf16[16,6,6,512]{3,2,1,0:T(8,128)(2,1)S(1)}, u32[]{:S(2)}, u32[]{:S(2)}) async-start(bf16[16,6,6,512]{3,2,1,0:T(8,128)(2,1)} %reshape.223), calls=%async_computation | async-start | bytes 1572864 | tf_op jit(solution)/shard_map/all_to_all | solution.py:44
  49.7 0.1 dynamic_slice.3
  49.8 0.1 iota_compare_fusion
  49.9 0.1 fusion.52
  49.9 1.3 %slice_bitcast_fusion = (bf16[6,256,256]{2,1,0:T(8,128)(2,1)}, bf16[6,256,256]{2,1,0:T(8,128)(2,1)}) fusion(bf16[6,2,256,256]{3,2,1,0:T(8,128)(2,1)S(1)} %copy-done.1), kind=kLoop, calls=%fused_computation.29 | loop fusion | bytes 3145728 | tf_op jit(solution)/shard_map/squeeze | solution.py:16
  51.2 18.2 %all-to-all-done = bf16[16,6,6,512]{3,2,1,0:T(8,128)(2,1)S(1)} async-done(((bf16[16,6,6,512]{3,2,1,0:T(8,128)(2,1)}), bf16[16,6,6,512]{3,2,1,0:T(8,128)(2,1)S(1)}, u32[]{:S(2)}, u32[]{:S(2)}) %all-to-all-start) | async-done | bytes 589856 | tf_op jit(solution)/shard_map/all_to_all | solution.py:44
  69.4 0.4 fusion.18
  69.7 2.4 %fusion.25 = bf16[96,6,512]{2,0,1:T(8,128)(2,1)S(1)} fusion(bf16[6,96,96]{2,1,0:T(8,128)(2,1)S(1)} %copy-done, bf16[6,512,96]{1,2,0:T(8,128)(2,1)S(1)} %fusion.18, bf16[6,256,256]{2,1,0:T(8,128)(2,1)} %get-tuple-element.10, bf16[6,256,256]{2,1,0:T(8,128)(2,1)S(1)} %fusion.52, bf16[6,256,256]{2,1,0:T(8,128)(2,1)} %get-tuple-element.9), kind=kOutput, calls=%fused_computation.25 | convolution fusion | flops 371785728 | bytes 3649536 | tf_op jit(solution)/shard_map/jlt,jld->tjd/dot_general | solution.py:57
  72.2 0.2 reshape.218
  72.4 1.0 copy.30
  73.3 4.4 %all-to-all-start.1 = ((bf16[16,6,6,512]{3,1,2,0:T(8,128)(2,1)}), bf16[16,6,6,512]{3,1,2,0:T(8,128)(2,1)S(1)}, u32[]{:S(2)}, u32[]{:S(2)}) async-start(bf16[16,6,6,512]{3,1,2,0:T(8,128)(2,1)} %copy.30), calls=%async_computation.1 | async-start | bytes 1572864 | tf_op jit(solution)/shard_map/all_to_all | solution.py:61
  77.8 2.9 %multiply_convert_fusion.1 = (bf16[1,96,1440]{2,1,0:T(8,128)(2,1)S(1)}, bf16[1,96,1440]{2,1,0:T(8,128)(2,1)S(1)}) fusion(s32[96]{0:T(128)S(1)} %copy-done.2, f32[96]{0:T(128)S(1)} %get-tuple-element.17, f32[96]{0:T(128)S(1)} %get-tuple-element.18), kind=kLoop, calls=%fused_computation.49 | loop fusion | flops 1797120 | bytes 554112 | tf_op jit(solution)/shard_map/convert.2
  80.6 16.7 %all-to-all-done.1 = bf16[16,6,6,512]{3,1,2,0:T(8,128)(2,1)S(1)} async-done(((bf16[16,6,6,512]{3,1,2,0:T(8,128)(2,1)}), bf16[16,6,6,512]{3,1,2,0:T(8,128)(2,1)S(1)}, u32[]{:S(2)}, u32[]{:S(2)}) %all-to-all-start.1) | async-done | bytes 589856 | tf_op jit(solution)/shard_map/all_to_all | solution.py:61
  97.4 0.3 reshape.224
  97.7 6.2 %fusion.3 = bf16[6,1440,256]{2,1,0:T(8,128)(2,1)} fusion(f32[256]{0:T(256)S(1)} %get-tuple-element.14, f32[256]{0:T(256)S(1)} %get-tuple-element.13, bf16[6,1440,256]{2,1,0:T(8,128)(2,1)} %param.5, bf16[1,96,1440]{2,1,0:T(8,128)(2,1)S(1)} %get-tuple-element.16, bf16[1,96,1440]{2,1,0:T(8,128)(2,1)S(1)} %get-tuple-element.15, ...), kind=kOutput, calls=%fused_computation.7 | convolution fusion | flops 868147200 | bytes 9992192 | tf_op jit(solution)/shard_map/akrc,rkn->anc/dot_general | solution.py:64
  (9 shorter events, 0.0 us)
Async XLA Ops:
  0.0 69.4 %copy-start = (bf16[6,96,96]{2,1,0:T(8,128)(2,1)S(1)}, bf16[6,96,96]{2,1,0:T(8,128)(2,1)}, u32[]{:S(2)}) copy-start(bf16[6,96,96]{2,1,0:T(8,128)(2,1)} %param.8) | copy-start | bytes 331780
  0.0 3.5 %copy-start.2 = (s32[96]{0:T(128)S(1)}, s32[96]{0:T(128)}, u32[]{:S(2)}) copy-start(s32[96]{0:T(128)} %param.7) | copy-start | bytes 1156
  0.0 28.8 %copy-start.3 = (f32[256]{0:T(256)S(1)}, f32[256]{0:T(256)}, u32[]{:S(2)}) copy-start(f32[256]{0:T(256)} %param.6) | copy-start | bytes 3076
  32.5 17.4 %copy-start.1 = (bf16[6,2,256,256]{3,2,1,0:T(8,128)(2,1)S(1)}, bf16[6,2,256,256]{3,2,1,0:T(8,128)(2,1)}, u32[]{:S(2)}) copy-start(bf16[6,2,256,256]{3,2,1,0:T(8,128)(2,1)} %param.9) | copy-start | bytes 4718596
  34.4 34.9 %all-to-all-start = ((bf16[16,6,6,512]{3,2,1,0:T(8,128)(2,1)}), bf16[16,6,6,512]{3,2,1,0:T(8,128)(2,1)S(1)}, u32[]{:S(2)}, u32[]{:S(2)}) async-start(bf16[16,6,6,512]{3,2,1,0:T(8,128)(2,1)} %reshape.223), calls=%async_computation | async-start | bytes 1572864 | tf_op jit(solution)/shard_map/all_to_all | solution.py:44
  73.3 24.0 %all-to-all-start.1 = ((bf16[16,6,6,512]{3,1,2,0:T(8,128)(2,1)}), bf16[16,6,6,512]{3,1,2,0:T(8,128)(2,1)S(1)}, u32[]{:S(2)}, u32[]{:S(2)}) async-start(bf16[16,6,6,512]{3,1,2,0:T(8,128)(2,1)} %copy.30), calls=%async_computation.1 | async-start | bytes 1572864 | tf_op jit(solution)/shard_map/all_to_all | solution.py:61
where the time goes:
time: 104 us
  waiting for transfers between devices  34.9 us (34%)
  blocking collectives  22.3 us (21%)
  starting transfers between devices  19.7 us (19%)
  matrix products  12.6 us (12%)
  other arithmetic  9.31 us (9%)
  local copies, waits for them, and re-layouts  4.87 us (5%)
    psum x1, blocking collectives, per_device(): total, squares = lax.psum((local_sum, local_sq), 'lat')  22.3 us
    all_to_all x1, waiting for transfers between devices, per_device(): lax.all_to_all(spectrum, 'lat', split_axis=0, concat_axis=1, tiled=True)[0]  18.2 us
    all_to_all x1, waiting for transfers between devices, per_device(): lax.all_to_all(back, 'lat', split_axis=0, concat_axis=2, tiled=True)[0]  16.7 us
    all_to_all x1, starting transfers between devices, per_device(): lax.all_to_all(spectrum, 'lat', split_axis=0, concat_axis=1, tiled=True)[0]  15.3 us
    dot_general x1, matrix products, per_device(): jnp.einsum('akrc,rkn->anc', returned, inverse, preferred_element_type=jnp...  6.16 us
    another operation x2, other arithmetic  5.69 us
    all_to_all x1, starting transfers between devices, per_device(): lax.all_to_all(back, 'lat', split_axis=0, concat_axis=2, tiled=True)[0]  4.42 us
    dot_general x1, matrix products, per_device(): jnp.einsum('anc,rdjn->dajrc', normed, forward, preferred_element_type=jnp...  3.65 us
  transfers between devices with their start and end apart: 2, of which 2 were waited for; matrix products, arithmetic and copies ran while one was open for 4% of the time, Pallas kernels for 0%

commit v1 on v0

--- a/solution.py
+++ b/solution.py
@@ -41,7 +41,10 @@
         * inv_root
     )
     spectrum = spectrum.astype(jnp.bfloat16).reshape(lat_count, lat_dev, slot_dev, 2 * chans)
-    arrived = lax.all_to_all(spectrum, "lat", split_axis=0, concat_axis=1, tiled=True)[0]
+    arrived = jnp.concatenate(
+        lax.all_to_all(jnp.stack(jnp.split(spectrum, lax.axis_size("lat"), axis=0)), "lat", 0, 0),
+        axis=1,
+    )[0]
     mine = lax.dynamic_slice_in_dim(slot_wave, lax.axis_index("lat") * slot_dev, slot_dev, 0)
     big = block_weight(mixing)
     lat_scale = math.sqrt(nlat / degs)

time: 104 us -> 115 us (1.11)
  local copies, waits for them, and re-layouts: 4.87 us -> 15 us
    unnamed x8 -> x23, local copies, waits for them, and re-layouts: 0.02 us -> 9.37 us
    reshape x2 -> x0, local copies, waits for them, and re-layouts: 1.88 us -> none  [per_device(): spectrum.astype(jnp.bfloat16)]
    split x0 -> x17, local copies, waits for them, and re-layouts: none -> 1.58 us  [per_device(): jnp.split(spectrum, lax.axis_size('lat'), axis=0)]
where the time goes in v1:
time: 115 us; the launch traced here: 114 us
  waiting for transfers between devices  34.9 us (30%)
  blocking collectives  22.3 us (19%)
  starting transfers between devices  19.7 us (17%)
  local copies, waits for them, and re-layouts  15 us (13%)
  matrix products  12.6 us (11%)
  other arithmetic  9.31 us (8%)
    psum x1, blocking collectives, per_device(): total, squares = lax.psum((local_sum, local_sq), 'lat')  22.3 us
    all_to_all x1, waiting for transfers between devices, per_device(): lax.all_to_all(jnp.stack(jnp.split(spectrum, lax.axis_size('lat'), axis=0...  18.2 us
    all_to_all x1, waiting for transfers between devices, per_device(): lax.all_to_all(back, 'lat', split_axis=0, concat_axis=2, tiled=True)[0]  16.7 us
    all_to_all x1, starting transfers between devices, per_device(): lax.all_to_all(jnp.stack(jnp.split(spectrum, lax.axis_size('lat'), axis=0...  15.3 us
    unnamed x23, local copies, waits for them, and re-layouts  9.37 us
    dot_general x1, matrix products, per_device(): jnp.einsum('akrc,rkn->anc', returned, inverse, preferred_element_type=jnp...  6.16 us
    another operation x2, other arithmetic  5.69 us
    all_to_all x1, starting transfers between devices, per_device(): lax.all_to_all(back, 'lat', split_axis=0, concat_axis=2, tiled=True)[0]  4.42 us
  transfers between devices with their start and end apart: 2, of which 2 were waited for; matrix products, arithmetic and copies ran while one was open for 4% of the time, Pallas kernels for 0%

profile of v1, /device:TPU:9, one launch (start us, length us, event | category | flops | bytes accessed | tf_op | source)
XLA Modules:
  0.0 114.3 jit_solution(14937252957286129905)
XLA Ops:
  0.0 3.5 %convert_reduce_fusion = (f32[256]{0:T(256)S(1)}, f32[256]{0:T(256)S(1)}) fusion(bf16[6,1440,256]{2,1,0:T(8,128)(2,1)} %param.5), kind=kLoop, calls=%fused_computation.2 | loop fusion | flops 8846848 | bytes 4425728 | tf_op jit(solution)/shard_map/reduce_sum | solution.py:28
  3.7 2.8 %cosine_convert_fusion = (bf16[1,16,6,1440]{3,1,2,0:T(8,128)(2,1)S(1)}, bf16[1,16,6,1440]{3,1,2,0:T(8,128)(2,1)S(1)}) fusion(s32[16,6]{0,1:T(8,128)S(1)} %copy.54), kind=kLoop, calls=%fused_computation.44 | loop fusion | flops 1658880 | bytes 553344 | tf_op jit(solution)/shard_map/convert
  6.5 22.3 %all-reduce = (f32[256]{0:T(256)S(1)}, f32[256]{0:T(256)S(1)}) all-reduce(f32[256]{0:T(256)S(1)} %get-tuple-element.6, f32[256]{0:T(256)S(1)} %get-tuple-element.5), channel_id=1, replica_groups=mesh['member'=2,'lat'=16] {'lat'}, use_global_device_ids=true, to_apply=%region_3.0 | all-reduce | flops 512 | bytes 4096 | tf_op jit(solution)/shard_map/psum | solution.py:30
  28.9 3.6 %fusion.26 = bf16[16,6,6,2,256]{4,0,1,2,3:T(8,128)(2,1)S(1)} fusion(f32[256]{0:T(256)S(1)} %get-tuple-element.30, f32[256]{0:T(256)S(1)} %get-tuple-element.29, bf16[6,1440,256]{2,1,0:T(8,128)(2,1)} %param.5, bf16[1,16,6,1440]{3,1,2,0:T(8,128)(2,1)S(1)} %get-tuple-element.28, bf16[1,16,6,1440]{3,1,2,0:T(8,128)(2,1)S(1)} %get-tuple-element.27), kind=kOutput, calls=%fused_computation.26 | convolution fusion | flops 859889664 | bytes 5568512 | tf_op jit(solution)/shard_map/anc,rdjn->dajrc/dot_general | solution.py:40
  32.5 0.9 fusion.53
  34.8 0.6 constant_dynamic-update-slice_fusion.15
  35.5 0.6 constant_dynamic-update-slice_fusion.14
  36.1 0.6 constant_dynamic-update-slice_fusion.13
  36.7 0.6 constant_dynamic-update-slice_fusion.12
  37.3 0.6 constant_dynamic-update-slice_fusion.11
  38.0 0.6 constant_dynamic-update-slice_fusion.10
  38.6 0.6 constant_dynamic-update-slice_fusion.9
  39.2 0.6 constant_dynamic-update-slice_fusion.8
  39.8 0.6 constant_dynamic-update-slice_fusion.7
  40.4 0.6 constant_dynamic-update-slice_fusion.6
  44.8 15.3 %all-to-all-start = ((bf16[16,1,6,6,512]{4,3,2,1,0:T(8,128)(2,1)}), bf16[16,1,6,6,512]{4,3,2,1,0:T(8,128)(2,1)S(1)}, u32[]{:S(2)}, u32[]{:S(2)}) async-start(bf16[16,1,6,6,512]{4,3,2,1,0:T(8,128)(2,1)} %constant_dynamic-update-slice_fusion), calls=%async_computation | async-start | bytes 1572864 | tf_op jit(solution)/shard_map/all_to_all | solution.py:45
  60.3 1.2 %slice_bitcast_fusion = (bf16[6,256,256]{2,1,0:T(8,128)(2,1)}, bf16[6,256,256]{2,1,0:T(8,128)(2,1)}) fusion(bf16[6,2,256,256]{3,2,1,0:T(8,128)(2,1)S(1)} %copy-done.1), kind=kLoop, calls=%fused_computation.29 | loop fusion | bytes 3145728 | tf_op jit(solution)/shard_map/squeeze | solution.py:16
  61.6 18.2 %all-to-all-done = bf16[16,1,6,6,512]{4,3,2,1,0:T(8,128)(2,1)S(1)} async-done(((bf16[16,1,6,6,512]{4,3,2,1,0:T(8,128)(2,1)}), bf16[16,1,6,6,512]{4,3,2,1,0:T(8,128)(2,1)S(1)}, u32[]{:S(2)}, u32[]{:S(2)}) %all-to-all-start) | async-done | bytes 589856 | tf_op jit(solution)/shard_map/all_to_all | solution.py:45
  80.1 2.4 %fusion.25 = bf16[96,6,512]{2,0,1:T(8,128)(2,1)S(1)} fusion(bf16[6,96,96]{2,1,0:T(8,128)(2,1)S(1)} %copy-done, bf16[6,512,96]{1,2,0:T(8,128)(2,1)S(1)} %fusion.18, bf16[6,256,256]{2,1,0:T(8,128)(2,1)} %get-tuple-element.10, bf16[6,256,256]{2,1,0:T(8,128)(2,1)S(1)} %fusion.52, bf16[6,256,256]{2,1,0:T(8,128)(2,1)} %get-tuple-element.9), kind=kOutput, calls=%fused_computation.25 | convolution fusion | flops 371785728 | bytes 3649536 | tf_op jit(solution)/shard_map/jlt,jld->tjd/dot_general | solution.py:60
  82.8 1.0 copy.75
  83.7 4.4 %all-to-all-start.1 = ((bf16[16,6,6,512]{3,1,2,0:T(8,128)(2,1)}), bf16[16,6,6,512]{3,1,2,0:T(8,128)(2,1)S(1)}, u32[]{:S(2)}, u32[]{:S(2)}) async-start(bf16[16,6,6,512]{3,1,2,0:T(8,128)(2,1)} %copy.75), calls=%async_computation.1 | async-start | bytes 1572864 | tf_op jit(solution)/shard_map/all_to_all | solution.py:64
  88.2 2.9 %multiply_convert_fusion.1 = (bf16[1,96,1440]{2,1,0:T(8,128)(2,1)S(1)}, bf16[1,96,1440]{2,1,0:T(8,128)(2,1)S(1)}) fusion(s32[96]{0:T(128)S(1)} %copy-done.2, f32[96]{0:T(128)S(1)} %get-tuple-element.33, f32[96]{0:T(128)S(1)} %get-tuple-element.34), kind=kLoop, calls=%fused_computation.49 | loop fusion | flops 1797120 | bytes 554112 | tf_op jit(solution)/shard_map/convert.2
  91.0 16.7 %all-to-all-done.1 = bf16[16,6,6,512]{3,1,2,0:T(8,128)(2,1)S(1)} async-done(((bf16[16,6,6,512]{3,1,2,0:T(8,128)(2,1)}), bf16[16,6,6,512]{3,1,2,0:T(8,128)(2,1)S(1)}, u32[]{:S(2)}, u32[]{:S(2)}) %all-to-all-start.1) | async-done | bytes 589856 | tf_op jit(solution)/shard_map/all_to_all | solution.py:64
  108.1 6.2 %fusion.3 = bf16[6,1440,256]{2,1,0:T(8,128)(2,1)} fusion(f32[256]{0:T(256)S(1)} %get-tuple-element.30, f32[256]{0:T(256)S(1)} %get-tuple-element.29, bf16[6,1440,256]{2,1,0:T(8,128)(2,1)} %param.5, bf16[1,96,1440]{2,1,0:T(8,128)(2,1)S(1)} %get-tuple-element.32, bf16[1,96,1440]{2,1,0:T(8,128)(2,1)S(1)} %get-tuple-element.31, ...), kind=kOutput, calls=%fused_computation.7 | convolution fusion | flops 868147200 | bytes 9992192 | tf_op jit(solution)/shard_map/akrc,rkn->anc/dot_general | solution.py:67
  (56 shorter events, 6.2 us)
Async XLA Ops:
  0.0 79.8 %copy-start = (bf16[6,96,96]{2,1,0:T(8,128)(2,1)S(1)}, bf16[6,96,96]{2,1,0:T(8,128)(2,1)}, u32[]{:S(2)}) copy-start(bf16[6,96,96]{2,1,0:T(8,128)(2,1)} %param.8) | copy-start | bytes 331780
  0.0 3.5 %copy-start.2 = (s32[96]{0:T(128)S(1)}, s32[96]{0:T(128)}, u32[]{:S(2)}) copy-start(s32[96]{0:T(128)} %param.7) | copy-start | bytes 1156
  0.0 28.8 %copy-start.3 = (f32[256]{0:T(256)S(1)}, f32[256]{0:T(256)}, u32[]{:S(2)}) copy-start(f32[256]{0:T(256)} %param.6) | copy-start | bytes 3076
  32.5 27.8 %copy-start.1 = (bf16[6,2,256,256]{3,2,1,0:T(8,128)(2,1)S(1)}, bf16[6,2,256,256]{3,2,1,0:T(8,128)(2,1)}, u32[]{:S(2)}) copy-start(bf16[6,2,256,256]{3,2,1,0:T(8,128)(2,1)} %param.9) | copy-start | bytes 4718596
  44.8 34.9 %all-to-all-start = ((bf16[16,1,6,6,512]{4,3,2,1,0:T(8,128)(2,1)}), bf16[16,1,6,6,512]{4,3,2,1,0:T(8,128)(2,1)S(1)}, u32[]{:S(2)}, u32[]{:S(2)}) async-start(bf16[16,1,6,6,512]{4,3,2,1,0:T(8,128)(2,1)} %constant_dynamic-update-slice_fusion), calls=%async_computation | async-start | bytes 1572864 | tf_op jit(solution)/shard_map/all_to_all | solution.py:45
  83.7 24.0 %all-to-all-start.1 = ((bf16[16,6,6,512]{3,1,2,0:T(8,128)(2,1)}), bf16[16,6,6,512]{3,1,2,0:T(8,128)(2,1)S(1)}, u32[]{:S(2)}, u32[]{:S(2)}) async-start(bf16[16,6,6,512]{3,1,2,0:T(8,128)(2,1)} %copy.75), calls=%async_computation.1 | async-start | bytes 1572864 | tf_op jit(solution)/shard_map/all_to_all | solution.py:64
